TPU v7x, 32 devices: a whole 2x2x4 slice. The times are simulated.
32 devices in a mesh: region: 4 (over z), depth: 2 (over y), member: 4 (over x, core).
Axes of the slice: x: 2, y: 2, z: 4, core: 2. Of those that a mesh axis runs over, the one named last changes fastest.
Arguments:
- ensemble: bfloat16 [14, 384, 4096], P('depth', 'member', 'region'), may hold values from -6 to 6
- obs_weights: float32 [14], P('depth'), may hold values from -1.5 to 1.5
- obs_tiles: int32 [2048], P('region'), may hold values from 0 to 1023
- obs_values: float32 [2048], P('region'), may hold values from -8 to 8
- obs_error: float32 [2048], P('region'), may hold values from 0.2 to 2
- obs_noise: float32 [384, 2048], P('member', 'region'), may hold values from -6 to 6
Outputs:
- analysis: bfloat16 [14, 384, 4096], P('depth', 'member', 'region')
- inflation: float32 [], replicated
Inputs may be any that keep to these rules, and one draw needn't show every extreme that they name: `obs_tiles`: the tile of the observation, counted within the 1024 tiles of the region whose block holds the observation.
All inputs are finite; a program needn't handle non-finite values.
Results may differ from a plain program's by a relative error of at most 0.011.
Values may be sent and summed in bfloat16 or wider, within the bound.
A program may use at most 64 MiB of HBM per device.

v0:
```python
import jax
import jax.numpy as jnp
from jax import lax
from jax.sharding import PartitionSpec as P

MEMBERS = 384
RADIUS = 1024


def extended(array, sides, width):
    for axis, dim in sides:
        peers, length = (lax.axis_size(axis), array.shape[dim])
        up = [(i, (i + 1) % peers) for i in range(peers - 1)]
        down = [(j, i) for i, j in up]
        last = lax.slice_in_dim(array, length - width, length, axis=dim)
        leading = lax.slice_in_dim(array, 0, width, axis=dim)
        before = lax.ppermute(last, axis, up)
        after = lax.ppermute(leading, axis, down)
        array = jnp.concatenate([before, array, after], axis=dim)
    return array


def regress(
    anomalies, own_anom, state_mean, obs_anom, perturbed, factor, obs_pos, first_tile, infl_root
):
    var_count = anomalies.shape[0]
    tile_count = anomalies.shape[2]
    block = 128

    def one_block(block_index, output):
        block_start = block_index * block
        slab = lax.dynamic_slice_in_dim(anomalies, block_start, block, 2)
        own_slab = lax.dynamic_slice_in_dim(own_anom, block_start, block, 2)
        means = lax.dynamic_slice_in_dim(state_mean, block_start, block, 1)
        covariance = jnp.einsum(
            "lmt,mj->ltj", slab, obs_anom, preferred_element_type=jnp.float32
        ) / (MEMBERS - 1)
        tile_pos = (first_tile + block_start + jnp.arange(block, dtype=jnp.int32)).astype(
            jnp.float32
        )
        closeness = jnp.maximum(0.0, 1.0 - jnp.abs(tile_pos[:, None] - obs_pos[None, :]) / RADIUS)
        kalman_gain = (covariance * (closeness * closeness * factor[None, :])[None]).astype(
            jnp.bfloat16
        )
        increment = jnp.einsum(
            "ltj,mj->lmt", kalman_gain, perturbed, preferred_element_type=jnp.float32
        )
        updated = (means[:, None, :] + infl_root * own_slab.astype(jnp.float32) + increment).astype(
            jnp.bfloat16
        )
        return lax.dynamic_update_slice_in_dim(output, updated, block_start, 2)

    output = jnp.zeros((var_count, perturbed.shape[0], tile_count), jnp.bfloat16)
    return lax.fori_loop(0, tile_count // block, one_block, output)


def shards(ensemble, obs_weights, obs_tiles, obs_values, obs_error, obs_noise):
    tile_count = ensemble.shape[2]
    own_members = ensemble.shape[1]
    obs_count = obs_tiles.shape[0]
    member_sum = jnp.sum(ensemble, axis=1, dtype=jnp.float32)
    picked = jnp.take(ensemble, obs_tiles, axis=2).astype(jnp.float32)
    partial_pred = jnp.einsum("lmk,l->mk", picked, obs_weights, precision=lax.Precision.HIGHEST)
    predicted = lax.psum(partial_pred, "depth")
    totals = lax.psum(
        (member_sum, jnp.sum(predicted, axis=0), jnp.sum(predicted * predicted, axis=0)), "member"
    )
    state_mean = totals[0] / MEMBERS
    obs_mean = totals[1] / MEMBERS
    obs_dev = predicted - obs_mean[None, :]
    obs_spread = (totals[2] - MEMBERS * obs_mean * obs_mean) / (MEMBERS - 1)
    innovation = obs_values - obs_mean
    global_sums = lax.psum(
        (jnp.sum(innovation * innovation), jnp.sum(obs_spread + obs_error)), "region"
    )
    inflation = global_sums[0] / global_sums[1]
    infl_root = jnp.sqrt(inflation)
    factor = inflation / (inflation * obs_spread + obs_error)
    obs_anom = obs_dev.astype(jnp.bfloat16)
    perturbed = (
        innovation[None, :] + jnp.sqrt(obs_error)[None, :] * obs_noise - infl_root * obs_dev
    ).astype(jnp.bfloat16)
    first_tile = lax.axis_index("region") * tile_count
    obs_pos = (first_tile + obs_tiles).astype(jnp.float32)
    stacked = jnp.concatenate([obs_anom, perturbed], axis=0)
    widened = extended(stacked, (("region", 1),), obs_count)
    near_anom = widened[:own_members]
    near_pert = widened[own_members:]
    scalars = jnp.stack([factor, obs_pos], axis=0)
    wide_scalars = extended(scalars, (("region", 1),), obs_count)
    near_factor = wide_scalars[0]
    near_pos = wide_scalars[1]
    anomalies = (ensemble.astype(jnp.float32) - state_mean[:, None, :]).astype(jnp.bfloat16)
    all_anom, all_obs_anom = (
        lax.all_gather(anomalies, "member", axis=1, tiled=True),
        lax.all_gather(near_anom, "member", axis=0, tiled=True),
    )
    analysis = regress(
        all_anom,
        anomalies,
        state_mean,
        all_obs_anom,
        near_pert,
        near_factor,
        near_pos,
        first_tile,
        infl_root,
    )
    return (analysis, inflation)


def solution(mesh):
    return jax.shard_map(
        shards,
        mesh=mesh,
        in_specs=(
            P("depth", "member", "region"),
            P("depth"),
            P("region"),
            P("region"),
            P("region"),
            P("member", "region"),
        ),
        out_specs=(P("depth", "member", "region"), P()),
        check_vma=False,
    )
```

profile of v0, /device:TPU:0, one launch (start us, length us, event | category | flops | bytes accessed | tf_op | source)
XLA Modules:
  0.0 185.1 jit_solution(7628334277064460269)
XLA Ops:
  7.2 0.0 all-reduce.4.cloned.1.call-start
  7.2 0.7 compare_and_fusion
  7.9 0.7 add_convert_fusion.1
  8.6 3.2 %copy.8 = bf16[7,96,1024]{1,0,2:T(8,128)(2,1)S(1)} copy(bf16[7,96,1024]{2,1,0:T(8,128)(2,1)} %param.8) | data formatting | bytes 2752512 | tf_op args[0]
  11.8 1.8 gather_fusion
  13.7 1.8 select_bitcast_fusion
  15.4 1.0 copy.9
  16.5 0.8 fusion.20
  17.3 0.7 copy.12
  18.0 0.0 all-gather.5.cloned.1.call-start
  18.1 0.3 convert_reduce_fusion
  18.4 25.0 %all-reduce.4.cloned.1.call-done = f32[96,512]{1,0:T(8,128)} async-done(((f32[96,512]{1,0:T(8,128)}), f32[96,512]{1,0:T(8,128)}) %all-reduce.4.cloned.1.call-update) | async-done | bytes 196624 | tf_op jit(solution)/shard_map/psum | solution.py:64
  43.3 1.0 multiply_reduce_fusion
  44.3 10.8 %all-reduce = (f32[7,1024]{1,0:T(8,128)S(1)}, f32[512]{0:T(512)S(1)}, f32[512]{0:T(512)S(1)}) all-reduce(f32[7,1024]{1,0:T(8,128)S(1)} %convert_reduce_fusion, f32[512]{0:T(512)S(1)} %get-tuple-element.188, f32[512]{0:T(512)S(1)} %get-tuple-element.187), channel_id=1, replica_groups=mesh['region'=4,'depth'=2,'member'=4] {'member'}, use_global_device_ids=true, to_apply=%region_1.2 | all-reduce | flops 8192 | bytes 65536 | tf_op jit(solution)/shard_map/psum | solution.py:65
  55.1 0.6 multiply_reduce_fusion.1
  55.7 12.3 %all-reduce.1 = (f32[]{:T(128)}, f32[]{:T(128)}) all-reduce(f32[]{:T(128)} %get-tuple-element.216, f32[]{:T(128)} %get-tuple-element.229), channel_id=1, replica_groups=mesh['region'=4,'depth'=2,'member'=4] {'region'}, use_global_device_ids=true, to_apply=%region_6.7 | all-reduce | flops 2 | bytes 16 | tf_op jit(solution)/shard_map/psum | solution.py:73
  69.5 1.0 subtract_convert_fusion.1
  70.5 1.3 collective-permute-start.1
  71.8 4.6 %collective-permute-start = (bf16[192,512]{1,0:T(8,128)(2,1)S(1)}, bf16[192,512]{1,0:T(8,128)(2,1)S(1)}, u32[]{:S(2)}, u32[]{:S(2)}) collective-permute-start(bf16[192,512]{1,0:T(8,128)(2,1)S(1)} %pad_maximum_fusion.1), channel_id=1, source_target_pairs={{0,8},{8,16},{16,24},{1,9},{9,17},{17,25},{2,10},{10,18},{18,26},{... | collective-permute-start | bytes 589832 | tf_op jit(solution)/shard_map/ppermute | solution.py:17
  76.4 1.7 collective-permute-done.1
  78.1 1.5 collective-permute-done
  79.6 0.8 fusion.23
  80.4 0.0 all-gather.3.cloned.1.call-start
  80.4 1.4 fusion.18
  81.9 1.3 collective-permute-start.3
  83.2 5.0 %collective-permute-start.2 = (f32[2,512]{1,0:T(2,128)S(1)}, f32[2,512]{1,0:T(2,128)S(1)}, u32[]{:S(2)}, u32[]{:S(2)}) collective-permute-start(f32[2,512]{1,0:T(2,128)S(1)} %pad_maximum_fusion.3), channel_id=1, source_target_pairs={{0,8},{8,16},{16,24},{1,9},{9,17},{17,25},{2,10},{10,18},{18,26},{... | collective-permute-start | bytes 12296 | tf_op jit(solution)/shard_map/ppermute | solution.py:17
  88.2 1.3 collective-permute-done.2
  89.6 7.4 %all-gather.5.cloned.1.call-done = bf16[384,1536]{1,0:T(8,128)(2,1)} async-done(((bf16[96,1536]{1,0:T(8,128)(2,1)}), bf16[384,1536]{1,0:T(8,128)(2,1)}) %all-gather.5.cloned.1.call-update) | async-done | bytes 1179664 | tf_op jit(solution)/shard_map/all_gather | solution.py:96
  97.0 44.1 %all-gather.3.cloned.1.call-done = bf16[7,384,1024]{2,1,0:T(8,128)(2,1)} async-done(((bf16[7,96,1024]{2,1,0:T(8,128)(2,1)}), bf16[7,384,1024]{2,1,0:T(8,128)(2,1)}) %all-gather.3.cloned.1.call-update) | async-done | bytes 5505040 | tf_op jit(solution)/shard_map/all_gather | solution.py:95
  141.0 0.2 broadcast_in_dim.28
  141.2 35.1 %while.13 = (s32[]{:T(128)}, bf16[7,96,1024]{2,1,0:T(8,128)(2,1)S(1)}, f32[7,1024]{1,0:T(8,128)S(1)}, f32[]{:T(128)}, bf16[7,96,1024]{2,1,0:T(8,128)(2,1)}, /*in...) while((s32[]{:T(128)}, ...), condition=%wide.region_12.13_spmd, body=%wide.region_11.12_spmd.sunk | while | flops 1325961472 | bytes 4130527 | solution.py:54
  141.3 0.3 multiply_multiply_fusion.2
  141.6 4.0 %fusion.33 = bf16[7,96,1024]{2,1,0:T(8,128)(2,1)S(1)} fusion(bf16[7,96,1024]{2,1,0:T(8,128)(2,1)S(1)} %get-tuple-element.314, s32[]{:T(128)S(6)} %select_n.27, f32[128,1536]{1,0:T(8,128)S(1)} %multiply_multiply_fusion.2, bf16[384,1536]{1,0:T(8,128)(2,1)} %get-tuple-element.335, bf16[7,384,1024]{2,1,0:T(8,128)(2,1)} %get-tuple-element.334, ...), kind=kOutput, calls=%fused_computation.7.clone.1 | convolution fusion | flops 1324388352 | bytes 3298816 | tf_op jit(solution)/shard_map/while/body/eval_jaxpr/ltj,mj->lmt/dot_general | solution.py:45
  145.7 0.3 multiply_multiply_fusion.2
  146.0 4.0 %fusion.33 = bf16[7,96,1024]{2,1,0:T(8,128)(2,1)S(1)} fusion(bf16[7,96,1024]{2,1,0:T(8,128)(2,1)S(1)} %get-tuple-element.314, s32[]{:T(128)S(6)} %select_n.27, f32[128,1536]{1,0:T(8,128)S(1)} %multiply_multiply_fusion.2, bf16[384,1536]{1,0:T(8,128)(2,1)} %get-tuple-element.335, bf16[7,384,1024]{2,1,0:T(8,128)(2,1)} %get-tuple-element.334, ...), kind=kOutput, calls=%fused_computation.7.clone.1 | convolution fusion | flops 1324388352 | bytes 3298816 | tf_op jit(solution)/shard_map/while/body/eval_jaxpr/ltj,mj->lmt/dot_general | solution.py:45
  150.1 0.3 multiply_multiply_fusion.2
  150.4 4.0 %fusion.33 = bf16[7,96,1024]{2,1,0:T(8,128)(2,1)S(1)} fusion(bf16[7,96,1024]{2,1,0:T(8,128)(2,1)S(1)} %get-tuple-element.314, s32[]{:T(128)S(6)} %select_n.27, f32[128,1536]{1,0:T(8,128)S(1)} %multiply_multiply_fusion.2, bf16[384,1536]{1,0:T(8,128)(2,1)} %get-tuple-element.335, bf16[7,384,1024]{2,1,0:T(8,128)(2,1)} %get-tuple-element.334, ...), kind=kOutput, calls=%fused_computation.7.clone.1 | convolution fusion | flops 1324388352 | bytes 3298816 | tf_op jit(solution)/shard_map/while/body/eval_jaxpr/ltj,mj->lmt/dot_general | solution.py:45
  154.5 0.3 multiply_multiply_fusion.2
  154.8 4.0 %fusion.33 = bf16[7,96,1024]{2,1,0:T(8,128)(2,1)S(1)} fusion(bf16[7,96,1024]{2,1,0:T(8,128)(2,1)S(1)} %get-tuple-element.314, s32[]{:T(128)S(6)} %select_n.27, f32[128,1536]{1,0:T(8,128)S(1)} %multiply_multiply_fusion.2, bf16[384,1536]{1,0:T(8,128)(2,1)} %get-tuple-element.335, bf16[7,384,1024]{2,1,0:T(8,128)(2,1)} %get-tuple-element.334, ...), kind=kOutput, calls=%fused_computation.7.clone.1 | convolution fusion | flops 1324388352 | bytes 3298816 | tf_op jit(solution)/shard_map/while/body/eval_jaxpr/ltj,mj->lmt/dot_general | solution.py:45
  158.9 0.3 multiply_multiply_fusion.2
  159.2 4.0 %fusion.33 = bf16[7,96,1024]{2,1,0:T(8,128)(2,1)S(1)} fusion(bf16[7,96,1024]{2,1,0:T(8,128)(2,1)S(1)} %get-tuple-element.314, s32[]{:T(128)S(6)} %select_n.27, f32[128,1536]{1,0:T(8,128)S(1)} %multiply_multiply_fusion.2, bf16[384,1536]{1,0:T(8,128)(2,1)} %get-tuple-element.335, bf16[7,384,1024]{2,1,0:T(8,128)(2,1)} %get-tuple-element.334, ...), kind=kOutput, calls=%fused_computation.7.clone.1 | convolution fusion | flops 1324388352 | bytes 3298816 | tf_op jit(solution)/shard_map/while/body/eval_jaxpr/ltj,mj->lmt/dot_general | solution.py:45
  163.3 0.3 multiply_multiply_fusion.2
  163.6 4.0 %fusion.33 = bf16[7,96,1024]{2,1,0:T(8,128)(2,1)S(1)} fusion(bf16[7,96,1024]{2,1,0:T(8,128)(2,1)S(1)} %get-tuple-element.314, s32[]{:T(128)S(6)} %select_n.27, f32[128,1536]{1,0:T(8,128)S(1)} %multiply_multiply_fusion.2, bf16[384,1536]{1,0:T(8,128)(2,1)} %get-tuple-element.335, bf16[7,384,1024]{2,1,0:T(8,128)(2,1)} %get-tuple-element.334, ...), kind=kOutput, calls=%fused_computation.7.clone.1 | convolution fusion | flops 1324388352 | bytes 3298816 | tf_op jit(solution)/shard_map/while/body/eval_jaxpr/ltj,mj->lmt/dot_general | solution.py:45
  167.7 0.3 multiply_multiply_fusion.2
  167.9 4.0 %fusion.33 = bf16[7,96,1024]{2,1,0:T(8,128)(2,1)S(1)} fusion(bf16[7,96,1024]{2,1,0:T(8,128)(2,1)S(1)} %get-tuple-element.314, s32[]{:T(128)S(6)} %select_n.27, f32[128,1536]{1,0:T(8,128)S(1)} %multiply_multiply_fusion.2, bf16[384,1536]{1,0:T(8,128)(2,1)} %get-tuple-element.335, bf16[7,384,1024]{2,1,0:T(8,128)(2,1)} %get-tuple-element.334, ...), kind=kOutput, calls=%fused_computation.7.clone.1 | convolution fusion | flops 1324388352 | bytes 3298816 | tf_op jit(solution)/shard_map/while/body/eval_jaxpr/ltj,mj->lmt/dot_general | solution.py:45
  172.1 0.3 multiply_multiply_fusion.2
  172.3 4.0 %fusion.33 = bf16[7,96,1024]{2,1,0:T(8,128)(2,1)S(1)} fusion(bf16[7,96,1024]{2,1,0:T(8,128)(2,1)S(1)} %get-tuple-element.314, s32[]{:T(128)S(6)} %select_n.27, f32[128,1536]{1,0:T(8,128)S(1)} %multiply_multiply_fusion.2, bf16[384,1536]{1,0:T(8,128)(2,1)} %get-tuple-element.335, bf16[7,384,1024]{2,1,0:T(8,128)(2,1)} %get-tuple-element.334, ...), kind=kOutput, calls=%fused_computation.7.clone.1 | convolution fusion | flops 1324388352 | bytes 3298816 | tf_op jit(solution)/shard_map/while/body/eval_jaxpr/ltj,mj->lmt/dot_general | solution.py:45
  176.4 1.1 copy-done.2
  (55 shorter events, 0.7 us)
Async XLA Ops:
  7.2 9.3 %copy-start = (f32[7]{0:T(128)S(1)}, f32[7]{0:T(128)}, u32[]{:S(2)}) copy-start(f32[7]{0:T(128)} %param.9) | copy-start | bytes 88
  7.2 36.1 %all-reduce.4.cloned.1.call-start = ((), (), s32[]{:S(2)}) async-start(), calls=%async_computation | async-start | bytes 393216 | tf_op jit(solution)/shard_map/psum | solution.py:64
  15.4 2.6 %copy-start.1 = (bf16[7,96,1024]{2,1,0:T(8,128)(2,1)S(1)}, bf16[7,96,1024]{2,1,0:T(8,128)(2,1)}, u32[]{:S(2)}) copy-start(bf16[7,96,1024]{2,1,0:T(8,128)(2,1)} %param.8) | copy-start | bytes 4128772
  16.5 38.6 %copy-start.4 = (f32[512]{0:T(512)S(1)}, f32[512]{0:T(512)}, u32[]{:S(2)}) copy-start(f32[512]{0:T(512)} %param.12) | copy-start | bytes 6148
  16.5 38.6 %copy-start.5 = (f32[512]{0:T(512)S(1)}, f32[512]{0:T(512)}, u32[]{:S(2)}) copy-start(f32[512]{0:T(512)} %param.11) | copy-start | bytes 6148
  17.3 52.2 %copy-start.3 = (f32[96,512]{1,0:T(8,128)S(1)}, f32[96,512]{1,0:T(8,128)}, u32[]{:S(2)}) copy-start(f32[96,512]{1,0:T(8,128)} %param.13) | copy-start | bytes 589828
  18.0 79.0 %all-gather.5.cloned.1.call-start = ((), (), s32[]{:S(2)}) async-start(), calls=%async_computation.2 | async-start | bytes 1474560 | tf_op jit(solution)/shard_map/all_gather | solution.py:96
  70.5 7.6 %collective-permute-start.1 = (bf16[192,512]{1,0:T(8,128)(2,1)S(1)}, bf16[192,512]{1,0:T(8,128)(2,1)S(1)}, u32[]{:S(2)}, u32[]{:S(2)}) collective-permute-start(bf16[192,512]{1,0:T(8,128)(2,1)S(1)} %pad_maximum_fusion.1), channel_id=1, source_target_pairs={{8,0},{16,8},{24,16},{9,1},{17,9},{25,17},{10,2},{18,10},{26,18},{... | collective-permute-start | bytes 589832 | tf_op jit(solution)/shard_map/ppermute | solution.py:18
  71.8 7.7 %collective-permute-start = (bf16[192,512]{1,0:T(8,128)(2,1)S(1)}, bf16[192,512]{1,0:T(8,128)(2,1)S(1)}, u32[]{:S(2)}, u32[]{:S(2)}) collective-permute-start(bf16[192,512]{1,0:T(8,128)(2,1)S(1)} %pad_maximum_fusion.1), channel_id=1, source_target_pairs={{0,8},{8,16},{16,24},{1,9},{9,17},{17,25},{2,10},{10,18},{18,26},{... | collective-permute-start | bytes 589832 | tf_op jit(solution)/shard_map/ppermute | solution.py:17
  80.4 60.7 %all-gather.3.cloned.1.call-start = ((), (), s32[]{:S(2)}) async-start(), calls=%async_computation.1 | async-start | bytes 6881280 | tf_op jit(solution)/shard_map/all_gather | solution.py:95
  81.9 6.3 %collective-permute-start.3 = (f32[2,512]{1,0:T(2,128)S(1)}, f32[2,512]{1,0:T(2,128)S(1)}, u32[]{:S(2)}, u32[]{:S(2)}) collective-permute-start(f32[2,512]{1,0:T(2,128)S(1)} %pad_maximum_fusion.3), channel_id=1, source_target_pairs={{8,0},{16,8},{24,16},{9,1},{17,9},{25,17},{10,2},{18,10},{26,18},{... | collective-permute-start | bytes 12296 | tf_op jit(solution)/shard_map/ppermute | solution.py:18
  83.2 6.3 %collective-permute-start.2 = (f32[2,512]{1,0:T(2,128)S(1)}, f32[2,512]{1,0:T(2,128)S(1)}, u32[]{:S(2)}, u32[]{:S(2)}) collective-permute-start(f32[2,512]{1,0:T(2,128)S(1)} %pad_maximum_fusion.3), channel_id=1, source_target_pairs={{0,8},{8,16},{16,24},{1,9},{9,17},{17,25},{2,10},{10,18},{18,26},{... | collective-permute-start | bytes 12296 | tf_op jit(solution)/shard_map/ppermute | solution.py:17
  176.3 1.1 copy-start.2
Sparse Core Ops, SparseCore 0:
  18.1 25.1 all-reduce.3
  80.5 16.4 all-gather.4
  99.1 41.8 all-gather.2
where the time goes:
time: 186 us; the launch traced here: 185 us
  waiting for transfers between devices  80.9 us (43%)
  matrix products  32.7 us (18%)
  blocking collectives  23.2 us (12%)
  between operations  16.5 us (9%)
  starting transfers between devices  12.3 us (7%)
  other arithmetic  10.1 us (5%)
  local copies, waits for them, and re-layouts  8.89 us (5%)
    all_gather x1, waiting for transfers between devices, shards(): lax.all_gather(anomalies, 'member', axis=1, tiled=True)  44.1 us
    dot_general x8, matrix products, one_block(): jnp.einsum('ltj,mj->lmt', kalman_gain, perturbed, preferred_element_type=...  31.9 us
    psum x1, waiting for transfers between devices, shards(): predicted = lax.psum(partial_pred, 'depth')  25 us
    psum x1, blocking collectives, shards(): lax.psum((jnp.sum(innovation * innovation), jnp.sum(obs_spread + obs_erro...  12.3 us
    psum x1, blocking collectives, shards(): lax.psum((member_sum, jnp.sum(predicted, axis=0), jnp.sum(predicted * pre...  10.8 us
    ppermute x2, starting transfers between devices, extended(): before = lax.ppermute(last, axis, up)  9.57 us
    all_gather x1, waiting for transfers between devices, shards(): lax.all_gather(near_anom, 'member', axis=0, tiled=True)  7.4 us
    unnamed x13, local copies, waits for them, and re-layouts  4.34 us
  transfers between devices with their start and end apart: 7, of which 6 were waited for; matrix products, arithmetic and copies ran while one was open for 1% of the time, Pallas kernels for 0%

commit v1 on v0

--- a/solution.py
+++ b/solution.py
@@ -5,6 +5,9 @@
 
 MEMBERS = 384
 RADIUS = 1024
+put_cycles_for = lambda patch, group_axis: jnp.concatenate(
+    jax.lax.all_gather(patch, axis_name=group_axis), 1
+)
 
 
 def extended(array, sides, width):
@@ -92,7 +95,7 @@
     near_pos = wide_scalars[1]
     anomalies = (ensemble.astype(jnp.float32) - state_mean[:, None, :]).astype(jnp.bfloat16)
     all_anom, all_obs_anom = (
-        lax.all_gather(anomalies, "member", axis=1, tiled=True),
+        put_cycles_for(anomalies, group_axis="member"),
         lax.all_gather(near_anom, "member", axis=0, tiled=True),
     )
     analysis = regress(

time: 186 us -> 162 us (0.87)
  waiting for transfers between devices: 80.9 us -> 57.4 us
  local copies, waits for them, and re-layouts: 8.89 us -> 15.4 us
  starting transfers between devices: 12.3 us -> 6.7 us
    all_gather x1, waiting for transfers between devices: 44.1 us -> 8.79 us  [jax.lax.all_gather(patch, axis_name=group_axis)]
    ppermute x2, waiting for transfers between devices: 1.7 us -> 8.59 us  [extended(): after = lax.ppermute(leading, axis, down)]
    reshape x0 -> x1, local copies, waits for them, and re-layouts: none -> 5.95 us  [jnp.concatenate(jax.lax.all_gather(patch, axis_name=group_axis), 1)]
    all_gather x1, waiting for transfers between devices: 7.4 us -> 13.1 us  [shards(): lax.all_gather(near_anom, 'member', axis=0, tiled=True)]
    ppermute x2, starting transfers between devices: 9.57 us -> 4 us  [extended(): before = lax.ppermute(last, axis, up)]
    unnamed x13 -> x15, local copies, waits for them, and re-layouts: 4.34 us -> 4.94 us
  transfers between devices with their start and end apart: 7 -> 7, of which waited for: 6 -> 6; matrix products, arithmetic and copies ran while one was open for 1% -> 5% of each run, Pallas kernels for 0% -> 0%
where the time goes in v1:
time: 162 us; the launch traced here: 161 us
  waiting for transfers between devices  57.4 us (35%)
  matrix products  32.6 us (20%)
  blocking collectives  23.2 us (14%)
  between operations  16.5 us (10%)
  local copies, waits for them, and re-layouts  15.4 us (10%)
  other arithmetic  9.15 us (6%)
  starting transfers between devices  6.7 us (4%)
    dot_general x8, matrix products, one_block(): jnp.einsum('ltj,mj->lmt', kalman_gain, perturbed, preferred_element_type=...  31.8 us
    psum x1, waiting for transfers between devices, shards(): predicted = lax.psum(partial_pred, 'depth')  25 us
    all_gather x1, waiting for transfers between devices, shards(): lax.all_gather(near_anom, 'member', axis=0, tiled=True)  13.1 us
    psum x1, blocking collectives, shards(): lax.psum((jnp.sum(innovation * innovation), jnp.sum(obs_spread + obs_erro...  12.4 us
    psum x1, blocking collectives, shards(): lax.psum((member_sum, jnp.sum(predicted, axis=0), jnp.sum(predicted * pre...  10.8 us
    all_gather x1, waiting for transfers between devices, jax.lax.all_gather(patch, axis_name=group_axis)  8.79 us
    ppermute x2, waiting for transfers between devices, extended(): after = lax.ppermute(leading, axis, down)  8.59 us
    reshape x1, local copies, waits for them, and re-layouts, jnp.concatenate(jax.lax.all_gather(patch, axis_name=group_axis), 1)  5.95 us
  transfers between devices with their start and end apart: 7, of which 6 were waited for; matrix products, arithmetic and copies ran while one was open for 5% of the time, Pallas kernels for 0%

profile of v1, /device:TPU:0, one launch (start us, length us, event | category | flops | bytes accessed | tf_op | source)
XLA Modules:
  0.0 161.4 jit_solution(3487958056996630153)
XLA Ops:
  7.2 0.7 compare_and_fusion
  7.9 0.7 add_convert_fusion.1
  8.6 3.2 %copy.15 = bf16[7,96,1024]{1,0,2:T(8,128)(2,1)S(1)} copy(bf16[7,96,1024]{2,1,0:T(8,128)(2,1)} %param.8) | data formatting | bytes 2752512 | tf_op args[0]
  11.8 1.8 %gather_fusion = bf16[512,7,96]{2,1,0:T(8,128)(2,1)S(1)} fusion(bf16[7,96,1024]{1,0,2:T(8,128)(2,1)S(1)} %copy.15, s32[1024]{0:T(1024)S(1)} %pad_clamp_fusion), kind=kCustom, calls=%fused_computation | custom fusion | bytes 1378304 | tf_op jit(solution)/shard_map/jit(_take)/gather | solution.py:65
  13.7 1.8 %select_bitcast_fusion = bf16[7,96,512]{1,0,2:T(8,128)(2,1)S(1)} fusion(bf16[512,7,96]{2,1,0:T(8,128)(2,1)S(1)} %gather_fusion, pred[512]{0:T(512)(128)(4,1)S(1)} %compare_and_fusion), kind=kLoop, calls=%fused_computation.17 | loop fusion | flops 344064 | bytes 1376768 | tf_op jit(solution)/shard_map/jit(_take)/select_n | solution.py:65
  15.4 1.0 copy.18
  16.5 0.8 fusion.20
  17.3 0.7 copy.22
  18.0 0.0 all-gather.6.cloned.1.call-start
  18.0 0.3 convert_reduce_fusion
  18.3 25.0 %all-reduce.4.cloned.1.call-done = f32[96,512]{1,0:T(8,128)} async-done(((f32[96,512]{1,0:T(8,128)}), f32[96,512]{1,0:T(8,128)}) %all-reduce.4.cloned.1.call-update) | async-done | bytes 196624 | tf_op jit(solution)/shard_map/psum | solution.py:67
  43.3 1.0 multiply_reduce_fusion
  44.2 10.8 %all-reduce = (f32[7,1024]{1,0:T(8,128)S(1)}, f32[512]{0:T(512)S(1)}, f32[512]{0:T(512)S(1)}) all-reduce(f32[7,1024]{1,0:T(8,128)S(1)} %convert_reduce_fusion, f32[512]{0:T(512)S(1)} %get-tuple-element.210, f32[512]{0:T(512)S(1)} %get-tuple-element.209), channel_id=1, replica_groups=mesh['region'=4,'depth'=2,'member'=4] {'member'}, use_global_device_ids=true, to_apply=%region_1.2 | all-reduce | flops 8192 | bytes 65536 | tf_op jit(solution)/shard_map/psum | solution.py:68
  55.1 1.4 fusion.18
  56.6 0.6 copy-done.5
  57.2 0.6 multiply_reduce_fusion.1
  57.9 12.4 %all-reduce.1 = (f32[]{:T(128)}, f32[]{:T(128)}) all-reduce(f32[]{:T(128)} %get-tuple-element.238, f32[]{:T(128)} %get-tuple-element.251), channel_id=1, replica_groups=mesh['region'=4,'depth'=2,'member'=4] {'region'}, use_global_device_ids=true, to_apply=%region_6.7 | all-reduce | flops 2 | bytes 16 | tf_op jit(solution)/shard_map/psum | solution.py:76
  71.7 0.1 subtract_convert_fusion.1
  71.8 1.3 collective-permute-start
  73.1 1.3 collective-permute-start.1
  74.4 1.9 %collective-permute-done = bf16[192,512]{1,0:T(8,128)(2,1)S(1)} collective-permute-done((bf16[192,512]{1,0:T(8,128)(2,1)S(1)}, bf16[192,512]{1,0:T(8,128)(2,1)S(1)}, u32[]{:S(2)}, u32[]{:S(2)}) %collective-permute-start) | collective-permute-done | bytes 196640 | tf_op jit(solution)/shard_map/ppermute | solution.py:20
  76.3 4.4 %collective-permute-done.1 = bf16[192,512]{1,0:T(8,128)(2,1)S(1)} collective-permute-done((bf16[192,512]{1,0:T(8,128)(2,1)S(1)}, bf16[192,512]{1,0:T(8,128)(2,1)S(1)}, u32[]{:S(2)}, u32[]{:S(2)}) %collective-permute-start.1) | collective-permute-done | bytes 196640 | tf_op jit(solution)/shard_map/ppermute | solution.py:21
  80.7 0.8 fusion.23
  81.5 2.7 %collective-permute-start.2 = (f32[2,512]{1,0:T(2,128)S(1)}, f32[2,512]{1,0:T(2,128)S(1)}, u32[]{:S(2)}, u32[]{:S(2)}) collective-permute-start(f32[2,512]{1,0:T(2,128)S(1)} %pad_maximum_fusion.3), channel_id=1, source_target_pairs={{0,8},{8,16},{16,24},{1,9},{9,17},{17,25},{2,10},{10,18},{18,26},{... | collective-permute-start | bytes 12296 | tf_op jit(solution)/shard_map/ppermute | solution.py:20
  84.2 1.3 collective-permute-start.3
  85.5 4.2 %collective-permute-done.3 = f32[2,512]{1,0:T(2,128)S(1)} collective-permute-done((f32[2,512]{1,0:T(2,128)S(1)}, f32[2,512]{1,0:T(2,128)S(1)}, u32[]{:S(2)}, u32[]{:S(2)}) %collective-permute-start.3) | collective-permute-done | bytes 4128 | tf_op jit(solution)/shard_map/ppermute | solution.py:21
  89.7 8.8 %all-gather.6.cloned.1.call-done = bf16[28,96,1024]{2,1,0:T(8,128)(2,1)} async-done(((bf16[7,96,1024]{2,1,0:T(8,128)(2,1)}), bf16[28,96,1024]{2,1,0:T(8,128)(2,1)}) %all-gather.6.cloned.1.call-update) | async-done | bytes 5505040 | tf_op jit(solution)/shard_map/all_gather | solution.py:9
  98.5 5.9 %copy.16 = bf16[7,4,96,1024]{3,2,1,0:T(8,128)(2,1)} copy(bf16[7,4,96,1024]{3,2,0,1:T(8,128)(2,1)} %bitcast.42) | data formatting | bytes 11010048 | tf_op jit(solution)/shard_map/reshape | solution.py:8
  104.5 13.1 %all-gather.4.cloned.1.call-done = bf16[384,1536]{1,0:T(8,128)(2,1)} async-done(((bf16[96,1536]{1,0:T(8,128)(2,1)}), bf16[384,1536]{1,0:T(8,128)(2,1)}) %all-gather.4.cloned.1.call-update) | async-done | bytes 1179664 | tf_op jit(solution)/shard_map/all_gather | solution.py:99
  117.6 0.2 broadcast_in_dim.28
  117.7 35.0 %while.13 = (s32[]{:T(128)}, bf16[7,96,1024]{2,1,0:T(8,128)(2,1)S(1)}, f32[7,1024]{1,0:T(8,128)S(1)}, f32[]{:T(128)}, bf16[7,96,1024]{2,1,0:T(8,128)(2,1)}, /*in...) while((s32[]{:T(128)}, ...), condition=%wide.region_12.13_spmd, body=%wide.region_11.12_spmd.sunk | while | flops 1325961472 | bytes 4130527 | solution.py:57
  117.8 0.3 multiply_multiply_fusion.2
  118.1 4.0 %fusion.33 = bf16[7,96,1024]{2,1,0:T(8,128)(2,1)S(1)} fusion(bf16[7,96,1024]{2,1,0:T(8,128)(2,1)S(1)} %get-tuple-element.336, s32[]{:T(128)S(6)} %select_n.27, f32[128,1536]{1,0:T(8,128)S(1)} %multiply_multiply_fusion.2, bf16[384,1536]{1,0:T(8,128)(2,1)} %get-tuple-element.357, bf16[7,384,1024]{2,1,0:T(8,128)(2,1)} %get-tuple-element.356, ...), kind=kOutput, calls=%fused_computation.7.clone.1 | convolution fusion | flops 1324388352 | bytes 3298816 | tf_op jit(solution)/shard_map/while/body/eval_jaxpr/ltj,mj->lmt/dot_general | solution.py:48
  122.2 0.3 multiply_multiply_fusion.2
  122.5 4.0 %fusion.33 = bf16[7,96,1024]{2,1,0:T(8,128)(2,1)S(1)} fusion(bf16[7,96,1024]{2,1,0:T(8,128)(2,1)S(1)} %get-tuple-element.336, s32[]{:T(128)S(6)} %select_n.27, f32[128,1536]{1,0:T(8,128)S(1)} %multiply_multiply_fusion.2, bf16[384,1536]{1,0:T(8,128)(2,1)} %get-tuple-element.357, bf16[7,384,1024]{2,1,0:T(8,128)(2,1)} %get-tuple-element.356, ...), kind=kOutput, calls=%fused_computation.7.clone.1 | convolution fusion | flops 1324388352 | bytes 3298816 | tf_op jit(solution)/shard_map/while/body/eval_jaxpr/ltj,mj->lmt/dot_general | solution.py:48
  126.6 0.3 multiply_multiply_fusion.2
  126.9 4.0 %fusion.33 = bf16[7,96,1024]{2,1,0:T(8,128)(2,1)S(1)} fusion(bf16[7,96,1024]{2,1,0:T(8,128)(2,1)S(1)} %get-tuple-element.336, s32[]{:T(128)S(6)} %select_n.27, f32[128,1536]{1,0:T(8,128)S(1)} %multiply_multiply_fusion.2, bf16[384,1536]{1,0:T(8,128)(2,1)} %get-tuple-element.357, bf16[7,384,1024]{2,1,0:T(8,128)(2,1)} %get-tuple-element.356, ...), kind=kOutput, calls=%fused_computation.7.clone.1 | convolution fusion | flops 1324388352 | bytes 3298816 | tf_op jit(solution)/shard_map/while/body/eval_jaxpr/ltj,mj->lmt/dot_general | solution.py:48
  131.0 0.3 multiply_multiply_fusion.2
  131.2 4.0 %fusion.33 = bf16[7,96,1024]{2,1,0:T(8,128)(2,1)S(1)} fusion(bf16[7,96,1024]{2,1,0:T(8,128)(2,1)S(1)} %get-tuple-element.336, s32[]{:T(128)S(6)} %select_n.27, f32[128,1536]{1,0:T(8,128)S(1)} %multiply_multiply_fusion.2, bf16[384,1536]{1,0:T(8,128)(2,1)} %get-tuple-element.357, bf16[7,384,1024]{2,1,0:T(8,128)(2,1)} %get-tuple-element.356, ...), kind=kOutput, calls=%fused_computation.7.clone.1 | convolution fusion | flops 1324388352 | bytes 3298816 | tf_op jit(solution)/shard_map/while/body/eval_jaxpr/ltj,mj->lmt/dot_general | solution.py:48
  135.3 0.3 multiply_multiply_fusion.2
  135.6 4.0 %fusion.33 = bf16[7,96,1024]{2,1,0:T(8,128)(2,1)S(1)} fusion(bf16[7,96,1024]{2,1,0:T(8,128)(2,1)S(1)} %get-tuple-element.336, s32[]{:T(128)S(6)} %select_n.27, f32[128,1536]{1,0:T(8,128)S(1)} %multiply_multiply_fusion.2, bf16[384,1536]{1,0:T(8,128)(2,1)} %get-tuple-element.357, bf16[7,384,1024]{2,1,0:T(8,128)(2,1)} %get-tuple-element.356, ...), kind=kOutput, calls=%fused_computation.7.clone.1 | convolution fusion | flops 1324388352 | bytes 3298816 | tf_op jit(solution)/shard_map/while/body/eval_jaxpr/ltj,mj->lmt/dot_general | solution.py:48
  139.7 0.3 multiply_multiply_fusion.2
  140.0 4.0 %fusion.33 = bf16[7,96,1024]{2,1,0:T(8,128)(2,1)S(1)} fusion(bf16[7,96,1024]{2,1,0:T(8,128)(2,1)S(1)} %get-tuple-element.336, s32[]{:T(128)S(6)} %select_n.27, f32[128,1536]{1,0:T(8,128)S(1)} %multiply_multiply_fusion.2, bf16[384,1536]{1,0:T(8,128)(2,1)} %get-tuple-element.357, bf16[7,384,1024]{2,1,0:T(8,128)(2,1)} %get-tuple-element.356, ...), kind=kOutput, calls=%fused_computation.7.clone.1 | convolution fusion | flops 1324388352 | bytes 3298816 | tf_op jit(solution)/shard_map/while/body/eval_jaxpr/ltj,mj->lmt/dot_general | solution.py:48
  144.1 0.3 multiply_multiply_fusion.2
  144.3 4.0 %fusion.33 = bf16[7,96,1024]{2,1,0:T(8,128)(2,1)S(1)} fusion(bf16[7,96,1024]{2,1,0:T(8,128)(2,1)S(1)} %get-tuple-element.336, s32[]{:T(128)S(6)} %select_n.27, f32[128,1536]{1,0:T(8,128)S(1)} %multiply_multiply_fusion.2, bf16[384,1536]{1,0:T(8,128)(2,1)} %get-tuple-element.357, bf16[7,384,1024]{2,1,0:T(8,128)(2,1)} %get-tuple-element.356, ...), kind=kOutput, calls=%fused_computation.7.clone.1 | convolution fusion | flops 1324388352 | bytes 3298816 | tf_op jit(solution)/shard_map/while/body/eval_jaxpr/ltj,mj->lmt/dot_general | solution.py:48
  148.4 0.3 multiply_multiply_fusion.2
  148.7 4.0 %fusion.33 = bf16[7,96,1024]{2,1,0:T(8,128)(2,1)S(1)} fusion(bf16[7,96,1024]{2,1,0:T(8,128)(2,1)S(1)} %get-tuple-element.336, s32[]{:T(128)S(6)} %select_n.27, f32[128,1536]{1,0:T(8,128)S(1)} %multiply_multiply_fusion.2, bf16[384,1536]{1,0:T(8,128)(2,1)} %get-tuple-element.357, bf16[7,384,1024]{2,1,0:T(8,128)(2,1)} %get-tuple-element.356, ...), kind=kOutput, calls=%fused_computation.7.clone.1 | convolution fusion | flops 1324388352 | bytes 3298816 | tf_op jit(solution)/shard_map/while/body/eval_jaxpr/ltj,mj->lmt/dot_general | solution.py:48
  152.7 1.1 copy-done.2
  (58 shorter events, 0.8 us)
Async XLA Ops:
  7.2 9.3 %copy-start = (f32[7]{0:T(128)S(1)}, f32[7]{0:T(128)}, u32[]{:S(2)}) copy-start(f32[7]{0:T(128)} %param.9) | copy-start | bytes 88
  7.2 36.1 %all-reduce.4.cloned.1.call-start = ((), (), s32[]{:S(2)}) async-start(), calls=%async_computation | async-start | bytes 393216 | tf_op jit(solution)/shard_map/psum | solution.py:67
  15.4 2.6 %copy-start.1 = (bf16[7,96,1024]{2,1,0:T(8,128)(2,1)S(1)}, bf16[7,96,1024]{2,1,0:T(8,128)(2,1)}, u32[]{:S(2)}) copy-start(bf16[7,96,1024]{2,1,0:T(8,128)(2,1)} %param.8) | copy-start | bytes 4128772
  18.0 80.5 %all-gather.6.cloned.1.call-start = ((), (), s32[]{:S(2)}) async-start(), calls=%async_computation.2 | async-start | bytes 6881280 | tf_op jit(solution)/shard_map/all_gather | solution.py:9
  56.5 0.7 copy-start.5
  56.5 0.7 copy-start.6
  56.5 15.1 %copy-start.3 = (f32[96,512]{1,0:T(8,128)S(1)}, f32[96,512]{1,0:T(8,128)}, u32[]{:S(2)}) copy-start(f32[96,512]{1,0:T(8,128)} %all-reduce.4.cloned.1.call-done) | copy-start | bytes 589828
  56.5 15.1 %copy-start.4 = (f32[96,512]{1,0:T(8,128)S(1)}, f32[96,512]{1,0:T(8,128)}, u32[]{:S(2)}) copy-start(f32[96,512]{1,0:T(8,128)} %param.13) | copy-start | bytes 589828
  56.6 61.0 %all-gather.4.cloned.1.call-start = ((), (), s32[]{:S(2)}) async-start(), calls=%async_computation.1 | async-start | bytes 1474560 | tf_op jit(solution)/shard_map/all_gather | solution.py:99
  71.8 4.5 %collective-permute-start = (bf16[192,512]{1,0:T(8,128)(2,1)S(1)}, bf16[192,512]{1,0:T(8,128)(2,1)S(1)}, u32[]{:S(2)}, u32[]{:S(2)}) collective-permute-start(bf16[192,512]{1,0:T(8,128)(2,1)S(1)} %pad_maximum_fusion.1), channel_id=1, source_target_pairs={{0,8},{8,16},{16,24},{1,9},{9,17},{17,25},{2,10},{10,18},{18,26},{... | collective-permute-start | bytes 589832 | tf_op jit(solution)/shard_map/ppermute | solution.py:20
  73.1 7.6 %collective-permute-start.1 = (bf16[192,512]{1,0:T(8,128)(2,1)S(1)}, bf16[192,512]{1,0:T(8,128)(2,1)S(1)}, u32[]{:S(2)}, u32[]{:S(2)}) collective-permute-start(bf16[192,512]{1,0:T(8,128)(2,1)S(1)} %pad_maximum_fusion.1), channel_id=1, source_target_pairs={{8,0},{16,8},{24,16},{9,1},{17,9},{25,17},{10,2},{18,10},{26,18},{... | collective-permute-start | bytes 589832 | tf_op jit(solution)/shard_map/ppermute | solution.py:21
  81.5 4.0 %collective-permute-start.2 = (f32[2,512]{1,0:T(2,128)S(1)}, f32[2,512]{1,0:T(2,128)S(1)}, u32[]{:S(2)}, u32[]{:S(2)}) collective-permute-start(f32[2,512]{1,0:T(2,128)S(1)} %pad_maximum_fusion.3), channel_id=1, source_target_pairs={{0,8},{8,16},{16,24},{1,9},{9,17},{17,25},{2,10},{10,18},{18,26},{... | collective-permute-start | bytes 12296 | tf_op jit(solution)/shard_map/ppermute | solution.py:20
  84.2 5.5 %collective-permute-start.3 = (f32[2,512]{1,0:T(2,128)S(1)}, f32[2,512]{1,0:T(2,128)S(1)}, u32[]{:S(2)}, u32[]{:S(2)}) collective-permute-start(f32[2,512]{1,0:T(2,128)S(1)} %pad_maximum_fusion.3), channel_id=1, source_target_pairs={{8,0},{16,8},{24,16},{9,1},{17,9},{25,17},{10,2},{18,10},{26,18},{... | collective-permute-start | bytes 12296 | tf_op jit(solution)/shard_map/ppermute | solution.py:21
  152.7 1.1 copy-start.2
Sparse Core Ops, SparseCore 0:
  18.1 25.1 all-reduce.3
  56.7 41.7 all-gather.5
  100.1 17.4 all-gather.3
